TPU v7x, 32 devices: a whole 2x2x4 slice. The times are simulated.
32 devices in a mesh: seq: 8 (over z, y), dp: 4 (over x, core).
Axes of the slice: x: 2, y: 2, z: 4, core: 2. Of those that a mesh axis runs over, the one named last changes fastest.
Arguments:
- attention_queries: bfloat16 [8, 2, 256, 4096], P('seq', None, 'dp'), parts along dimension 2, may hold values from -5.5 to 5.5
- attention_keys: bfloat16 [8, 2, 256, 512], P('seq', None, 'dp'), parts along dimension 2, may hold values from -7.5 to 7.5
- attention_values: bfloat16 [8, 2, 256, 512], P('seq', None, 'dp'), parts along dimension 2, may hold values from -6 to 6
- attention_output: bfloat16 [8, 2, 256, 4096], P('seq', None, 'dp'), parts along dimension 2, may hold values from -6 to 6
- output_gradient: bfloat16 [8, 2, 256, 4096], P('seq', None, 'dp'), parts along dimension 2, may hold values from -48 to 48
- logsumexp_rows: float32 [8, 2, 256, 32], P('seq', None, 'dp'), parts along dimension 2, as said below
Outputs:
- grad_query: float32 [8, 2, 256, 4096], P('seq', None, 'dp'), parts along dimension 2
- key_gradient: float32 [8, 2, 256, 512], P('seq', None, 'dp'), parts along dimension 2
- value_gradient: float32 [8, 2, 256, 512], P('seq', None, 'dp'), parts along dimension 2
There are 4 independent parts, one for each index of `dp`. A program takes and returns all parts, laid end to end along the dimension named above; each array names one. Nothing has to cross between parts.
Inputs may be any that keep to these rules, and one draw needn't show every extreme that they name: logsumexp_rows[i, h] is the logarithm of the sum over key positions t <= i of exp(scores[h, i, t]), computed from attention_queries and attention_keys in float32.
All inputs are finite; a program needn't handle non-finite values.
Results may differ from a plain program's by a relative error of at most 0.0003.
Values may be sent and summed in bfloat16 or wider, within the bound.
A program may use at most 128 MiB of HBM per device.

v0:
```python
import jax
import jax.numpy as jnp
from jax import lax
from jax.sharding import PartitionSpec as P

HEAD_SIZE = 128


def split_parts(values):
    high_part = values.astype(jnp.bfloat16)
    back_value = lax.optimization_barrier(high_part).astype(jnp.float32)
    rest_part = (values - back_value).astype(jnp.bfloat16)
    return (high_part, rest_part)


def tile_grads(key_tile, value_tile, query_tile, grad_tile, log_rows, deltas, allowed, scaling):
    scores = scaling * jnp.einsum(
        "hkd,hqd->hkq", key_tile, query_tile, preferred_element_type=jnp.float32
    )
    weights = jnp.where(allowed[None], jnp.exp(scores - log_rows[:, None, :]), 0.0)
    weights_high, weights_rest = split_parts(weights)
    weight_grad = jnp.einsum(
        "hkd,hqd->hkq", value_tile, grad_tile, preferred_element_type=jnp.float32
    )
    score_grad = weights * (weight_grad - deltas[:, None, :])
    score_high, score_rest = split_parts(score_grad)
    value_part = jnp.einsum(
        "hkq,hqd->hkd", weights_high, grad_tile, preferred_element_type=jnp.float32
    ) + jnp.einsum("hkq,hqd->hkd", weights_rest, grad_tile, preferred_element_type=jnp.float32)
    key_part = scaling * (
        jnp.einsum("hkq,hqd->hkd", score_high, query_tile, preferred_element_type=jnp.float32)
        + jnp.einsum("hkq,hqd->hkd", score_rest, query_tile, preferred_element_type=jnp.float32)
    )
    query_part = scaling * (
        jnp.einsum("hkq,hkd->hqd", score_high, key_tile, preferred_element_type=jnp.float32)
        + jnp.einsum("hkq,hkd->hqd", score_rest, key_tile, preferred_element_type=jnp.float32)
    )
    return (query_part, key_part, value_part)


def sweep(step_fn, carried, pieces, offset):
    shards = pieces[0].shape[0]
    stride = 4

    def advance(iteration, running):
        groups = tuple(
            (lax.dynamic_slice_in_dim(member, iteration * stride, stride, 0) for member in pieces)
        )
        return step_fn(running, groups, offset + iteration * stride)

    return lax.fori_loop(0, shards // stride, advance, carried)


def add_rows(total_buffer, addend, offset):
    current = lax.dynamic_slice_in_dim(total_buffer, offset, addend.shape[0], 0)
    return lax.dynamic_update_slice_in_dim(total_buffer, current + addend, offset, 0)


def body(
    attention_queries,
    attention_keys,
    attention_values,
    attention_output,
    output_gradient,
    logsumexp_rows,
):
    scaling = HEAD_SIZE ** (-0.5)
    block_rows = attention_queries.shape[2]
    heads_kv = attention_keys.shape[3] // HEAD_SIZE
    group_size = attention_queries.shape[3] // (heads_kv * HEAD_SIZE)
    query_rows = group_size * block_rows
    feature_width = heads_kv * HEAD_SIZE
    seq_size = lax.axis_size("seq")
    device = lax.axis_index("seq")

    def by_heads(blocks):
        shaped = blocks[0].reshape(2, block_rows, heads_kv, group_size, HEAD_SIZE)
        return shaped.transpose(2, 0, 3, 1, 4).reshape(heads_kv, 2, query_rows, HEAD_SIZE)

    def place(owner, half, within):
        if half == 0:
            return owner * block_rows + within
        return (2 * seq_size - 1 - owner) * block_rows + within

    query_heads = by_heads(attention_queries)
    grad_heads = by_heads(output_gradient)
    row_delta = jnp.sum(
        grad_heads.astype(jnp.float32) * by_heads(attention_output).astype(jnp.float32), axis=-1
    )
    shaped = logsumexp_rows[0].reshape(2, block_rows, heads_kv, group_size)
    row_logs = shaped.transpose(2, 0, 3, 1).reshape(heads_kv, 2, query_rows)
    within_rows = jnp.arange(query_rows, dtype=jnp.int32) % block_rows
    key_within = jnp.arange(block_rows, dtype=jnp.int32)
    own_query_pos = (place(device, 0, within_rows), place(device, 1, within_rows))

    def keys_step(running, groups, offset):
        shards = groups[0].shape[0]
        key_group = groups[0].reshape(shards, 2, block_rows, heads_kv, HEAD_SIZE)
        value_group = groups[1].reshape(shards, 2, block_rows, heads_kv, HEAD_SIZE)
        owners = offset + jnp.arange(shards, dtype=jnp.int32)
        key_tile = key_group.transpose(3, 0, 1, 2, 4).reshape(
            heads_kv, shards * 2 * block_rows, HEAD_SIZE
        )
        value_tile = value_group.transpose(3, 0, 1, 2, 4).reshape(
            heads_kv, shards * 2 * block_rows, HEAD_SIZE
        )
        key_pos = jnp.stack(
            [
                place(owners[:, None], 0, key_within[None, :]),
                place(owners[:, None], 1, key_within[None, :]),
            ],
            1,
        ).reshape(shards * 2 * block_rows)
        query_pos = jnp.concatenate(own_query_pos, 0)
        allowed = key_pos[:, None] <= query_pos[None, :]
        parts = tile_grads(
            key_tile,
            value_tile,
            query_heads.reshape(heads_kv, 2 * query_rows, HEAD_SIZE),
            grad_heads.reshape(heads_kv, 2 * query_rows, HEAD_SIZE),
            row_logs.reshape(heads_kv, 2 * query_rows),
            row_delta.reshape(heads_kv, 2 * query_rows),
            allowed,
            scaling,
        )
        query_sum = running[0] + parts[0].reshape(running[0].shape)
        key_rows = (
            parts[1]
            .reshape(heads_kv, shards, 2, block_rows, HEAD_SIZE)
            .transpose(1, 2, 3, 0, 4)
            .reshape(shards, 2, block_rows, feature_width)
        )
        value_rows = (
            parts[2]
            .reshape(heads_kv, shards, 2, block_rows, HEAD_SIZE)
            .transpose(1, 2, 3, 0, 4)
            .reshape(shards, 2, block_rows, feature_width)
        )
        return (
            query_sum,
            add_rows(running[1], key_rows, offset),
            add_rows(running[2], value_rows, offset),
        )

    query_init = jnp.zeros((heads_kv, 2, query_rows, HEAD_SIZE), jnp.float32)
    key_total = jnp.zeros((seq_size, 2, block_rows, feature_width), jnp.float32)
    grads_init = (query_init, key_total, key_total)
    gathered = (
        lax.all_gather(attention_keys, "seq", axis=0, tiled=True),
        lax.all_gather(attention_values, "seq", axis=0, tiled=True),
    )
    results = sweep(keys_step, grads_init, gathered, 0)
    key_out, value_out = (
        lax.psum_scatter(results[1], "seq", scatter_dimension=0, tiled=True),
        lax.psum_scatter(results[2], "seq", scatter_dimension=0, tiled=True),
    )
    query_out = (
        results[0]
        .reshape(heads_kv, 2, group_size, block_rows, HEAD_SIZE)
        .transpose(1, 3, 0, 2, 4)
        .reshape(1, 2, block_rows, heads_kv * group_size * HEAD_SIZE)
    )
    return (query_out, key_out, value_out)


def solution(mesh):
    placed = (
        P("seq", None, "dp", None),
        P("seq", None, "dp", None),
        P("seq", None, "dp", None),
        P("seq", None, "dp", None),
        P("seq", None, "dp", None),
        P("seq", None, "dp", None),
    )
    return jax.shard_map(
        body,
        mesh=mesh,
        in_specs=placed,
        out_specs=(
            P("seq", None, "dp", None),
            P("seq", None, "dp", None),
            P("seq", None, "dp", None),
        ),
        check_vma=False,
    )
```

profile of v0, /device:TPU:0, one launch (start us, length us, event | category | flops | bytes accessed | tf_op | source)
XLA Modules:
  0.0 309.4 jit_solution(10748815907861812985)
XLA Ops:
  7.2 0.7 all-gather.3.cloned.1.call-update
  8.0 0.7 all-gather.5.cloned.1.call-update
  8.7 0.8 copy.42
  9.6 1.5 copy.51
  11.1 1.4 copy.43
  12.8 1.4 copy.41
  14.5 0.9 fusion.11
  15.6 37.6 %all-gather.3.cloned.1.call-done = bf16[8,2,64,512]{3,2,1,0:T(8,128)(2,1)} async-done(((bf16[1,2,64,512]{3,2,1,0:T(8,128)(2,1)}), bf16[8,2,64,512]{3,2,1,0:T(8,128)(2,1)}) %all-gather.3.cloned.1.call-update) | async-done | bytes 1048592 | tf_op jit(solution)/shard_map/all_gather | solution.py:149
  53.1 41.1 %all-gather.5.cloned.1.call-done = bf16[8,2,64,512]{3,2,1,0:T(8,128)(2,1)} async-done(((bf16[1,2,64,512]{3,2,1,0:T(8,128)(2,1)}), bf16[8,2,64,512]{3,2,1,0:T(8,128)(2,1)}) %all-gather.5.cloned.1.call-update) | async-done | bytes 1048592 | tf_op jit(solution)/shard_map/all_gather | solution.py:150
  94.3 1.6 broadcast_in_dim.52.clone
  95.9 1.6 broadcast_in_dim.52
  97.5 66.6 %while.22 = (s32[]{:T(128)}, f32[4,2,512,128]{3,2,1,0:T(8,128)}, f32[8,2,64,512]{3,2,1,0:T(8,128)}, f32[8,2,64,512]{3,2,1,0:T(8,128)}, s32[1024]{0:T(1024)S(1)},...) while((s32[]{:T(128)}, f32[4,2,512,128]{3,2,1,0:T(8,128)}, ...), condition=%wide.wide.region_2.3_spmd.clone.clone, body=%wide.wide.region_1.2_spmd.clone.clone.sunk | while | flops 4345037824 | bytes 193053136 | solution.py:51
  97.8 0.4 broadcast_compare_fusion.3
  98.2 1.1 constant_dynamic-slice_fusion.6
  99.5 1.1 constant_dynamic-slice_fusion.7
  100.9 3.6 %fusion.89 = (bf16[4,512,1024]{2,1,0:T(8,128)(2,1)S(1)}, f32[4,512,1024]{2,1,0:T(8,128)S(1)}) fusion(f32[4,1024]{1,0:T(4,128)S(1)} %get-tuple-element.611, pred[512,1024]{1,0:T(8,128)(4,1)S(1)} %broadcast_compare_fusion.3, bf16[4,512,128]{2,1,0:T(8,128)(2,1)S(1)} %bitcast.156, bf16[4,1024,128]{2,1,0:T(8,128)(2,1)} %bitcast.151), kind=kOutput, calls=%fused_computation.5.clone.clone.1 | convolution fusion | flops 545259520 | bytes 14696448 | tf_op jit(solution)/shard_map/while/body/eval_jaxpr/hkd,hqd->hkq/dot_general | solution.py:17
  104.5 4.6 %fusion.92 = f32[4,512,128]{2,1,0:T(8,128)S(1)} fusion(bf16[4,1024,128]{2,1,0:T(8,128)(2,1)} %bitcast.148, bf16[4,512,1024]{2,1,0:T(8,128)(2,1)S(1)} %get-tuple-element.565, f32[4,512,1024]{2,1,0:T(8,128)S(1)} %get-tuple-element.562, f32[4,1024]{1,0:T(4,128)S(1)} %get-tuple-element.611, pred[512,1024]{1,0:T(8,128)(4,1)S(1)} %broadcast_compare_fusion.3), kind=kOutput, calls=%fused_computation.6.clone.clone.1 | convolution fusion | flops 549453824 | bytes 15220736 | tf_op jit(solution)/shard_map/while/body/eval_jaxpr/hkq,hqd->hkd/dot_general | solution.py:29
  109.1 2.5 convolution_add_fusion.4
  111.6 5.4 %fusion.90 = (bf16[4,512,1024]{2,1,0:T(8,128)(2,1)S(1)}, f32[4,512,1024]{2,1,0:T(8,128)S(1)}) fusion(f32[4,1024]{1,0:T(4,128)S(1)} %bitcast.170, bf16[4,512,128]{2,1,0:T(8,128)(2,1)S(1)} %bitcast.162, bf16[4,1024,128]{2,1,0:T(8,128)(2,1)} %bitcast.148, f32[4,1024]{1,0:T(4,128)S(1)} %get-tuple-element.611, f32[4,512,1024]{2,1,0:T(8,128)} %copy-done, ...), kind=kOutput, calls=%fused_computation.39.clone.clone.1 | convolution fusion | flops 549453824 | bytes 23101440 | tf_op jit(solution)/shard_map/while/body/eval_jaxpr/hkd,hqd->hkq/dot_general | solution.py:22
  117.1 2.5 fusion.93
  119.6 2.7 fusion.94
  122.3 0.5 fusion.95
  122.8 1.3 copy-done.3
  124.1 0.7 copy-done.5
  124.8 1.6 fusion.91
  126.5 1.9 add_multiply_fusion.3
  128.4 1.7 select_add_fusion.3
  130.3 0.4 broadcast_compare_fusion.3
  130.7 1.1 constant_dynamic-slice_fusion.6
  132.1 1.1 constant_dynamic-slice_fusion.7
  133.4 3.6 %fusion.89 = (bf16[4,512,1024]{2,1,0:T(8,128)(2,1)S(1)}, f32[4,512,1024]{2,1,0:T(8,128)S(1)}) fusion(f32[4,1024]{1,0:T(4,128)S(1)} %get-tuple-element.611, pred[512,1024]{1,0:T(8,128)(4,1)S(1)} %broadcast_compare_fusion.3, bf16[4,512,128]{2,1,0:T(8,128)(2,1)S(1)} %bitcast.156, bf16[4,1024,128]{2,1,0:T(8,128)(2,1)} %bitcast.151), kind=kOutput, calls=%fused_computation.5.clone.clone.1 | convolution fusion | flops 545259520 | bytes 14696448 | tf_op jit(solution)/shard_map/while/body/eval_jaxpr/hkd,hqd->hkq/dot_general | solution.py:17
  137.0 4.6 %fusion.92 = f32[4,512,128]{2,1,0:T(8,128)S(1)} fusion(bf16[4,1024,128]{2,1,0:T(8,128)(2,1)} %bitcast.148, bf16[4,512,1024]{2,1,0:T(8,128)(2,1)S(1)} %get-tuple-element.565, f32[4,512,1024]{2,1,0:T(8,128)S(1)} %get-tuple-element.562, f32[4,1024]{1,0:T(4,128)S(1)} %get-tuple-element.611, pred[512,1024]{1,0:T(8,128)(4,1)S(1)} %broadcast_compare_fusion.3), kind=kOutput, calls=%fused_computation.6.clone.clone.1 | convolution fusion | flops 549453824 | bytes 15220736 | tf_op jit(solution)/shard_map/while/body/eval_jaxpr/hkq,hqd->hkd/dot_general | solution.py:29
  141.6 2.5 convolution_add_fusion.4
  144.2 5.4 %fusion.90 = (bf16[4,512,1024]{2,1,0:T(8,128)(2,1)S(1)}, f32[4,512,1024]{2,1,0:T(8,128)S(1)}) fusion(f32[4,1024]{1,0:T(4,128)S(1)} %bitcast.170, bf16[4,512,128]{2,1,0:T(8,128)(2,1)S(1)} %bitcast.162, bf16[4,1024,128]{2,1,0:T(8,128)(2,1)} %bitcast.148, f32[4,1024]{1,0:T(4,128)S(1)} %get-tuple-element.611, f32[4,512,1024]{2,1,0:T(8,128)} %copy-done, ...), kind=kOutput, calls=%fused_computation.39.clone.clone.1 | convolution fusion | flops 549453824 | bytes 23101440 | tf_op jit(solution)/shard_map/while/body/eval_jaxpr/hkd,hqd->hkq/dot_general | solution.py:22
  149.6 2.5 fusion.93
  152.1 2.7 fusion.94
  154.8 0.5 fusion.95
  155.4 1.3 copy-done.3
  156.7 0.7 copy-done.5
  157.3 1.6 fusion.91
  159.0 1.9 add_multiply_fusion.3
  160.9 3.2 %select_add_fusion.3 = f32[4,2,512,128]{3,2,1,0:T(8,128)} fusion(f32[4,2,512,128]{3,2,1,0:T(8,128)S(1)} %bitcast.155, f32[4,2,512,128]{3,2,1,0:T(8,128)} %get-tuple-element.585, pred[]{:T(512)S(6)} %compare.5), kind=kLoop, calls=%fused_computation.8.clone.clone.1 | loop fusion | flops 1048576 | bytes 6291457 | tf_op jit(solution)/shard_map/while/body/eval_jaxpr/add | solution.py:126
  164.2 0.5 reduce-scatter.3.cloned.1.call-update
  164.8 1.0 copy-done.1
  165.8 2.6 copy.56
  168.3 2.7 reshape.235
  171.1 60.4 %reduce-scatter.5.cloned.1.call-done = f32[1,2,64,512]{3,2,1,0:T(8,128)} async-done(((f32[8,2,64,512]{3,2,1,0:T(8,128)}), f32[1,2,64,512]{3,2,1,0:T(8,128)}) %reduce-scatter.5.cloned.1.call-update) | async-done | bytes 262160 | tf_op jit(solution)/shard_map/reduce_scatter | solution.py:155
  231.5 71.4 %reduce-scatter.3.cloned.1.call-done = f32[1,2,64,512]{3,2,1,0:T(8,128)} async-done(((f32[8,2,64,512]{3,2,1,0:T(8,128)}), f32[1,2,64,512]{3,2,1,0:T(8,128)}) %reduce-scatter.3.cloned.1.call-update) | async-done | bytes 262160 | tf_op jit(solution)/shard_map/reduce_scatter | solution.py:154
  (58 shorter events, 2.5 us)
Async XLA Ops:
  7.2 5.4 %copy-start.7 = (bf16[1,2,64,4096]{3,2,1,0:T(8,128)(2,1)S(1)}, bf16[1,2,64,4096]{3,2,1,0:T(8,128)(2,1)}, u32[]{:S(2)}) copy-start(bf16[1,2,64,4096]{3,2,1,0:T(8,128)(2,1)} %param.8) | copy-start | bytes 3145732
  7.2 46.0 %all-gather.3.cloned.1.call-start = ((), (), s32[]{:S(2)}) async-start(), calls=%async_computation.2 | async-start | bytes 1179648 | tf_op jit(solution)/shard_map/all_gather | solution.py:149
  7.9 86.4 %all-gather.5.cloned.1.call-start = ((), (), s32[]{:S(2)}) async-start(), calls=%async_computation.3 | async-start | bytes 1179648 | tf_op jit(solution)/shard_map/all_gather | solution.py:150
  8.7 222.8 %reduce-scatter.5.cloned.1.call-start = ((), (), s32[]{:S(2)}) async-start(), calls=%async_computation.5 | async-start | bytes 2359296 | tf_op jit(solution)/shard_map/reduce_scatter | solution.py:155
  9.5 4.7 %copy-start.8 = (f32[4,2,8,64]{3,2,1,0:T(8,128)}, f32[4,2,8,64]{3,2,1,0:T(8,128)S(1)}, u32[]{:S(2)}) copy-start(f32[4,2,8,64]{3,2,1,0:T(8,128)S(1)} %copy.42) | copy-start | bytes 49156
  9.6 4.6 %copy-start.6 = (bf16[1,2,64,4096]{3,2,1,0:T(8,128)(2,1)S(1)}, bf16[1,2,64,4096]{3,2,1,0:T(8,128)(2,1)}, u32[]{:S(2)}) copy-start(bf16[1,2,64,4096]{3,2,1,0:T(8,128)(2,1)} %param.11) | copy-start | bytes 3145732
  104.5 4.6 %copy-start = (f32[4,512,1024]{2,1,0:T(8,128)}, f32[4,512,1024]{2,1,0:T(8,128)S(1)}, u32[]{:S(2)}) copy-start(f32[4,512,1024]{2,1,0:T(8,128)S(1)} %get-tuple-element.562) | copy-start | bytes 25165828 | tf_op jit(solution)/shard_map/while
  119.5 2.8 copy-start.2
  119.6 2.8 copy-start.4
  122.8 1.3 copy-start.3
  122.8 2.0 copy-start.5
  137.0 4.6 %copy-start = (f32[4,512,1024]{2,1,0:T(8,128)}, f32[4,512,1024]{2,1,0:T(8,128)S(1)}, u32[]{:S(2)}) copy-start(f32[4,512,1024]{2,1,0:T(8,128)S(1)} %get-tuple-element.562) | copy-start | bytes 25165828 | tf_op jit(solution)/shard_map/while
  152.1 2.8 copy-start.2
  152.1 2.8 copy-start.4
  155.3 1.3 copy-start.3
  155.3 2.0 copy-start.5
  164.2 1.6 copy-start.1
  164.2 138.7 %reduce-scatter.3.cloned.1.call-start = ((), (), s32[]{:S(2)}) async-start(), calls=%async_computation.4 | async-start | bytes 2359296 | tf_op jit(solution)/shard_map/reduce_scatter | solution.py:154
Sparse Core Ops, SparseCore 0:
  10.1 42.9 all-gather.2
  55.3 38.9 all-gather.4
  164.3 67.1 reduce-scatter.4
  235.4 67.3 reduce-scatter.2
where the time goes:
time: 310 us; the launch traced here: 309 us
  waiting for transfers between devices  212 us (68%)
  matrix products  49.8 us (16%)
  local copies, waits for them, and re-layouts  25 us (8%)
  between operations  13.8 us (4%)
  other arithmetic  7.82 us (3%)
    reduce_scatter x1, waiting for transfers between devices, body(): lax.psum_scatter(results[1], 'seq', scatter_dimension=0, tiled=True)  71.4 us
    reduce_scatter x1, waiting for transfers between devices, body(): lax.psum_scatter(results[2], 'seq', scatter_dimension=0, tiled=True)  60.4 us
    all_gather x1, waiting for transfers between devices, body(): lax.all_gather(attention_values, 'seq', axis=0, tiled=True)  41.1 us
    all_gather x1, waiting for transfers between devices, body(): lax.all_gather(attention_keys, 'seq', axis=0, tiled=True)  37.6 us
    dot_general x2, matrix products, tile_grads(): jnp.einsum('hkd,hqd->hkq', value_tile, grad_tile, preferred_element_type=...  10.8 us
    dot_general x2, matrix products, tile_grads(): jnp.einsum('hkq,hqd->hkd', weights_rest, grad_tile, preferred_element_typ...  9.19 us
    dot_general x2, matrix products, tile_grads(): jnp.einsum('hkd,hqd->hkq', key_tile, query_tile, preferred_element_type=j...  7.18 us
    unnamed x14, local copies, waits for them, and re-layouts  6.64 us
  transfers between devices with their start and end apart: 4, of which 4 were waited for; matrix products, arithmetic and copies ran while one was open for 4% of the time, Pallas kernels for 0%

commit v1 on v0

v1 whole, which is shorter than its diff:
```python
import functools

import jax
import jax.numpy as jnp
from jax import lax
from jax.experimental import pallas as pl
from jax.experimental.pallas import tpu as pltpu
from jax.sharding import PartitionSpec as P

HEAD_SIZE = 128
LOG2E = 1.4426950408889634
MESH = pl.DeviceIdType.MESH
KEYS, VALUES = 0, 1
RIGHT, LEFT = 0, 1


def ring_place(index, size):
    return jnp.where(index % 2 == 0, index // 2, size - 1 - index // 2)


def ring_index(place, size):
    return jnp.where(place < size // 2, 2 * place, 2 * (size - 1 - place) + 1)


def split_parts(values):
    high = values.astype(jnp.bfloat16)
    rest = (values - high.astype(jnp.float32)).astype(jnp.bfloat16)
    return jnp.concatenate([high, rest], axis=0)


def dot_rows(a, b):
    return lax.dot_general(a, b, (((1,), (1,)), ((), ())), preferred_element_type=jnp.float32)


def dot(a, b):
    return jnp.dot(a, b, preferred_element_type=jnp.float32)


def kernel(
    n,
    q_ref,
    k_ref,
    v_ref,
    o_ref,
    g_ref,
    lse_ref,
    gq_ref,
    gk_ref,
    gv_ref,
    qs,
    gs,
    delta,
    dqt,
    kv,
    part,
    landed,
    ag_send,
    ag_recv,
    rs_send,
    rs_recv,
):
    half = n // 2
    rows = k_ref.shape[2]
    kv_heads = k_ref.shape[3] // HEAD_SIZE
    group = q_ref.shape[3] // k_ref.shape[3]
    wide = group * rows
    scaling = HEAD_SIZE ** (-0.5)
    me = lax.axis_index("seq")
    place = ring_place(me, n)
    right = ring_index(lax.rem(place + 1, n), n)
    left = ring_index(lax.rem(place + n - 1, n), n)
    target = (right, left)

    barrier = pltpu.get_barrier_semaphore()
    for neighbour in (left, right):
        pl.semaphore_signal(barrier, inc=1, device_id={"seq": neighbour}, device_id_type=MESH)
    pl.semaphore_wait(barrier, 2)

    def gather_copy(way, what, distance, own):
        arrives = n - distance if way == RIGHT else distance
        held = lax.rem(n + 1 - distance, n) if way == RIGHT else distance - 1
        source = (k_ref, v_ref)[what].at[0] if own else kv.at[held, what]
        return pltpu.make_async_remote_copy(
            src_ref=source,
            dst_ref=kv.at[arrives, what],
            send_sem=ag_send.at[way, distance - 1, what],
            recv_sem=ag_recv.at[way, distance - 1, what],
            device_id={"seq": target[way]},
            device_id_type=MESH,
        )

    def sum_copy(what, step, block):
        slot = n - 1 - step if what == KEYS else 1 + step
        return pltpu.make_async_remote_copy(
            src_ref=part.at[what, slot, block],
            dst_ref=landed.at[what, step, block],
            send_sem=rs_send.at[what, step, block],
            recv_sem=rs_recv.at[what, step, block],
            device_id={"seq": target[what]},
            device_id_type=MESH,
        )

    for what in (KEYS, VALUES):
        for way in (RIGHT, LEFT):
            if half > 1 or what == way:
                gather_copy(way, what, 1, True).start()

    def prepare(g, _):
        for a in range(2):
            products = []
            for j in range(group):
                columns = pl.ds(pl.multiple_of((g * group + j) * HEAD_SIZE, HEAD_SIZE), HEAD_SIZE)
                grad = g_ref[0, a, :, columns]
                qs[g, a, pl.ds(j * rows, rows), :] = q_ref[0, a, :, columns]
                gs[g, a, pl.ds(j * rows, rows), :] = grad
                products.append(grad.astype(jnp.float32) * o_ref[0, a, :, columns].astype(jnp.float32))
            turned = jnp.transpose(jnp.concatenate(products, axis=0))
            delta[g, a] = jnp.sum(turned, axis=0, keepdims=True)
            dqt[g, a] = jnp.zeros((HEAD_SIZE, wide), jnp.float32)
        return 0

    lax.fori_loop(0, kv_heads, prepare, 0)

    def unit(key_tile, value_tile, g, a, masked):
        queries, grads = qs[g, a], gs[g, a]
        scores = dot_rows(key_tile, queries)
        weights = jnp.exp2(scores * (scaling * LOG2E) - lse_ref[g, a])
        if masked:
            key_row = lax.broadcasted_iota(jnp.int32, (rows, wide), 0)
            query_row = lax.broadcasted_iota(jnp.int32, (rows, wide), 1) % rows
            weights = jnp.where(key_row <= query_row, weights, 0.0)
        value_part = dot(split_parts(weights), grads)
        score_grad = weights * (dot_rows(value_tile, grads) - delta[g, a])
        split = split_parts(score_grad)
        key_part = dot(split, queries)
        keys_turned = jnp.transpose(jnp.concatenate([key_tile, key_tile], axis=0))
        query_part = dot(keys_turned, split)
        return key_part[:rows] + key_part[rows:], value_part[:rows] + value_part[rows:], query_part

    def columns_of(g):
        return pl.ds(pl.multiple_of(g * HEAD_SIZE, HEAD_SIZE), HEAD_SIZE)

    def shard(slot):
        later = ring_index(lax.rem(place + slot, n), n) > me
        pick = jnp.where(later, 1, 0)

        def head(g, _):
            cols = columns_of(g)
            early = unit(kv[slot, KEYS, 0, :, cols], kv[slot, VALUES, 0, :, cols], g, 1, False)
            other = unit(kv[slot, KEYS, pick, :, cols], kv[slot, VALUES, pick, :, cols], g, pick, False)
            for what in (KEYS, VALUES):
                part[what, slot, 0, :, cols] = early[what] + jnp.where(later, 0.0, other[what])
                part[what, slot, 1, :, cols] = jnp.where(later, other[what], 0.0)
            dqt[g, 1] += early[2]
            dqt[g, pick] += other[2]
            return 0

        lax.fori_loop(0, kv_heads, head, 0)


    def own_shard():
        def head(g, _):
            cols = columns_of(g)
            tiles = [(k_ref[0, b, :, cols], v_ref[0, b, :, cols]) for b in range(2)]
            first = unit(*tiles[0], g, 0, True)
            across = unit(*tiles[0], g, 1, False)
            last = unit(*tiles[1], g, 1, True)
            for what in (KEYS, VALUES):
                part[what, 0, 0, :, cols] = first[what] + across[what]
                part[what, 0, 1, :, cols] = last[what]
            dqt[g, 0] += first[2]
            dqt[g, 1] += across[2] + last[2]
            return 0

        lax.fori_loop(0, kv_heads, head, 0)

    def receive(distance):
        gather_copy(RIGHT, KEYS, distance, False).wait_recv()
        gather_copy(LEFT, VALUES, distance, False).wait_recv()
        gather_copy(RIGHT, VALUES, distance, False).wait_recv()
        gather_copy(LEFT, KEYS, distance, False).wait_recv()

    def send_sums(step, first):
        for block in range(2):
            for what in (KEYS, VALUES):
                if not first:
                    slot = n - 1 - step if what == KEYS else 1 + step
                    sum_copy(what, step - 1, block).wait_recv()
                    part[what, slot, block] += landed[what, step - 1, block]
                sum_copy(what, step, block).start()

    def near(step, first):
        receive(step + 1)

        gather_copy(RIGHT, KEYS, step + 2, False).start()
        gather_copy(LEFT, VALUES, step + 2, False).start()

        @pl.when(step + 2 < half)
        def _():
            gather_copy(RIGHT, VALUES, step + 2, False).start()
            gather_copy(LEFT, KEYS, step + 2, False).start()

        def side(which, _):
            shard(jnp.where(which == 0, n - 1 - step, 1 + step))
            return 0

        lax.fori_loop(0, 2, side, 0)
        send_sums(step, first)

    if half > 1:
        near(0, True)

        def middle(step, _):
            near(step, False)
            return 0

        lax.fori_loop(1, half - 1, middle, 0)

    gather_copy(RIGHT, KEYS, half, False).wait_recv()
    gather_copy(LEFT, VALUES, half, False).wait_recv()
    shard(half)
    send_sums(half - 1, half == 1)

    own_shard()
    for a in range(2):
        def write(g, _):
            turned = jnp.transpose(dqt[g, a]) * scaling
            for j in range(group):
                columns = pl.ds(pl.multiple_of((g * group + j) * HEAD_SIZE, HEAD_SIZE), HEAD_SIZE)
                gq_ref[0, a, :, columns] = turned[j * rows : (j + 1) * rows]
            return 0

        lax.fori_loop(0, kv_heads, write, 0)

    def far(step, _):
        send_sums(step, False)
        return 0

    lax.fori_loop(half, n - 1, far, 0)
    for block in range(2):
        for what in (KEYS, VALUES):
            sum_copy(what, n - 2, block).wait_recv()
            total = part[what, 0, block] + landed[what, n - 2, block]
            if what == KEYS:
                gk_ref[0, block] = total * scaling
            else:
                gv_ref[0, block] = total

    def sent(step, _):
        for block in range(2):
            for what in (KEYS, VALUES):
                sum_copy(what, step, block).wait_send()
        return 0

    lax.fori_loop(0, n - 1, sent, 0)

    def passed(distance, _):
        gather_copy(RIGHT, KEYS, distance, False).wait_send()
        gather_copy(LEFT, VALUES, distance, False).wait_send()
        gather_copy(RIGHT, VALUES, distance, False).wait_send()
        gather_copy(LEFT, KEYS, distance, False).wait_send()
        return 0

    lax.fori_loop(1, half, passed, 0)
    gather_copy(RIGHT, KEYS, half, False).wait_send()
    gather_copy(LEFT, VALUES, half, False).wait_send()


def body(queries, keys, values, output, gradient, logsumexp):
    n = lax.axis_size("seq")
    rows = keys.shape[2]
    kv_heads = keys.shape[3] // HEAD_SIZE
    group = queries.shape[3] // keys.shape[3]
    wide = group * rows
    lse = logsumexp[0].reshape(2, rows, kv_heads, group).transpose(2, 0, 3, 1)
    lse = (lse * LOG2E).reshape(kv_heads, 2, 1, wide)
    vmem = pl.BlockSpec(memory_space=pltpu.VMEM)
    pair = (2, rows, keys.shape[3])
    return pl.pallas_call(
        functools.partial(kernel, n),
        out_shape=(
            jax.ShapeDtypeStruct(queries.shape, jnp.float32),
            jax.ShapeDtypeStruct(keys.shape, jnp.float32),
            jax.ShapeDtypeStruct(values.shape, jnp.float32),
        ),
        in_specs=[vmem] * 6,
        out_specs=(vmem, vmem, vmem),
        scratch_shapes=[
            pltpu.VMEM((kv_heads, 2, wide, HEAD_SIZE), jnp.bfloat16),
            pltpu.VMEM((kv_heads, 2, wide, HEAD_SIZE), jnp.bfloat16),
            pltpu.VMEM((kv_heads, 2, 1, wide), jnp.float32),
            pltpu.VMEM((kv_heads, 2, HEAD_SIZE, wide), jnp.float32),
            pltpu.VMEM((n, 2) + pair, jnp.bfloat16),
            pltpu.VMEM((2, n) + pair, jnp.float32),
            pltpu.VMEM((2, n - 1) + pair, jnp.float32),
            pltpu.SemaphoreType.DMA((2, n // 2, 2)),
            pltpu.SemaphoreType.DMA((2, n // 2, 2)),
            pltpu.SemaphoreType.DMA((2, n - 1, 2)),
            pltpu.SemaphoreType.DMA((2, n - 1, 2)),
        ],
        compiler_params=pltpu.CompilerParams(
            collective_id=0, has_side_effects=True, vmem_limit_bytes=64_000_000
        ),
    )(queries, keys, values, output, gradient, lse)


def solution(mesh):
    spec = P("seq", None, "dp", None)
    return jax.shard_map(
        body, mesh=mesh, in_specs=(spec,) * 6, out_specs=(spec,) * 3, check_vma=False
    )
```

time: 310 us -> 81.3 us (0.26)
  waiting for transfers between devices: 212 us -> 0 us
  Pallas kernels: 0 us -> 74.4 us
  matrix products: 49.8 us -> 0 us
  local copies, waits for them, and re-layouts: 25 us -> 5.27 us
  between operations: 13.8 us -> 0.66 us
  other arithmetic: 7.82 us -> 0.76 us
    reduce_scatter x2 -> x0, waiting for transfers between devices: 132 us -> none  [the longest x1 71.4 us: body(): lax.psum_scatter(results[1], 'seq', scatter_dimension=0, tiled=True)]
    all_gather x2 -> x0, waiting for transfers between devices: 78.7 us -> none  [the longest x1 41.1 us: body(): lax.all_gather(attention_values, 'seq', axis=0, tiled=True)]
    pallas_call x0 -> x1, Pallas kernels: none -> 74.4 us  [body(): pl.pallas_call(functools.partial(kernel, n), out_shape=(jax.ShapeDtypeStr...]
    dot_general x16 -> x0, matrix products: 49.8 us -> none  [the longest x2 10.8 us: tile_grads(): jnp.einsum('hkd,hqd->hkq', value_tile, grad_tile, preferred_element_type=...]
    add x7 -> x0, other arithmetic: 5.21 us -> none  [the longest x2 4.91 us: keys_step(): query_sum = running[0] + parts[0].reshape(running[0].shape)]
    reshape x6 -> x1, local copies, waits for them, and re-layouts: 5.81 us -> 0.69 us  [body(): lse = (lse * LOG2E).reshape(kv_heads, 2, 1, wide)]
    dynamic_slice x4 -> x0, local copies, waits for them, and re-layouts: 4.36 us -> none  [advance(): lax.dynamic_slice_in_dim(member, iteration * stride, stride, 0)]
    while x22 -> x0, local copies, waits for them, and re-layouts: 4.01 us -> none
  transfers between devices with their start and end apart: 4 -> 0, of which waited for: 4 -> 0; matrix products, arithmetic and copies ran while one was open for 4% -> 0% of each run, Pallas kernels for 0% -> 0%
where the time goes in v1:
time: 81.3 us; the launch traced here: 81.1 us
  Pallas kernels  74.4 us (92%)
  local copies, waits for them, and re-layouts  5.27 us (6%)
    pallas_call x1, Pallas kernels, body(): pl.pallas_call(functools.partial(kernel, n), out_shape=(jax.ShapeDtypeStr...  74.4 us
    unnamed x7, local copies, waits for them, and re-layouts  4.58 us

profile of v1, /device:TPU:0, one launch (start us, length us, event | category | flops | bytes accessed | tf_op | source)
XLA Modules:
  0.0 81.1 jit_solution(6668678417634184534)
XLA Ops:
  0.6 0.8 copy_bitcast_fusion
  1.4 0.7 reshape.11.lse_ref
  2.1 74.4 %shard_map.85 = (f32[1,2,64,4096]{3,2,1,0:T(8,128)}, f32[1,2,64,512]{3,2,1,0:T(8,128)}, f32[1,2,64,512]{3,2,1,0:T(8,128)}) custom-call(bf16[1,2,64,4096]{3,2,1,0:T(8,128)(2,1)} %q_ref.1, bf16[1,2,64,512]{3,2,1,0:T(8,128)(2,1)} %k_ref.1, bf16[1,2,64,512]{3,2,1,0:T(8,128)(2,1)} %v_ref.1, bf16[1,2,64,4096]{3,2,1,0:T(8,128)(2,1)} %o_ref.1, ...), custom_call_target="tpu_custom_call" | custom-call | tf_op jit(solution)/shard_map/pallas_call | solution.py:279
  76.5 0.0 copy-start.1
  76.5 0.0 copy-start
  76.5 3.2 %copy.14 = f32[1,2,64,4096]{3,2,1,0:T(8,128)} copy(f32[1,2,64,4096]{3,2,1,0:T(8,128)} %get-tuple-element.6) | data formatting | bytes 4194304
  79.7 0.0 copy-done.1
  79.7 0.7 copy.15
  80.4 0.0 copy-done
  80.4 0.7 copy.16
Async XLA Ops:
  76.5 3.2 %copy-start.1 = (f32[1,2,64,512]{3,2,1,0:T(8,128)S(1)}, f32[1,2,64,512]{3,2,1,0:T(8,128)}, u32[]{:S(2)}) copy-start(f32[1,2,64,512]{3,2,1,0:T(8,128)} %get-tuple-element.7) | copy-start | bytes 786436
  76.5 3.9 %copy-start = (f32[1,2,64,512]{3,2,1,0:T(8,128)S(1)}, f32[1,2,64,512]{3,2,1,0:T(8,128)}, u32[]{:S(2)}) copy-start(f32[1,2,64,512]{3,2,1,0:T(8,128)} %get-tuple-element.8) | copy-start | bytes 786436

commit v2 on v1

--- a/solution.py
+++ b/solution.py
@@ -12,6 +12,7 @@
 MESH = pl.DeviceIdType.MESH
 KEYS, VALUES = 0, 1
 RIGHT, LEFT = 0, 1
+ORDER = ((RIGHT, KEYS), (LEFT, VALUES), (RIGHT, VALUES), (LEFT, KEYS))
 
 
 def ring_place(index, size):
@@ -50,6 +51,7 @@
     qs,
     gs,
     delta,
+    lse,
     dqt,
     kv,
     part,
@@ -100,14 +102,24 @@
             device_id_type=MESH,
         )
 
-    for what in (KEYS, VALUES):
-        for way in (RIGHT, LEFT):
-            if half > 1 or what == way:
-                gather_copy(way, what, 1, True).start()
+    for way, what in ORDER:
+        if half > 1 or what == way:
+            gather_copy(way, what, 1, True).start()
+
+    def pass_on(step):
+        for way, what in ORDER:
+            gather_copy(way, what, step + 1, False).wait_recv()
+            onward = gather_copy(way, what, step + 2, False)
+            if what == way:
+                onward.start()
+            else:
+                pl.when(step + 2 < half)(onward.start)
 
     def prepare(g, _):
         for a in range(2):
             products = []
+            logs = lse_ref[0, a, pl.ds(pl.multiple_of(g * group, group), group), :] * LOG2E
+            lse[g, a] = jnp.concatenate([logs[j : j + 1] for j in range(group)], axis=1)
             for j in range(group):
                 columns = pl.ds(pl.multiple_of((g * group + j) * HEAD_SIZE, HEAD_SIZE), HEAD_SIZE)
                 grad = g_ref[0, a, :, columns]
@@ -119,12 +131,15 @@
             dqt[g, a] = jnp.zeros((HEAD_SIZE, wide), jnp.float32)
         return 0
 
-    lax.fori_loop(0, kv_heads, prepare, 0)
+    lax.fori_loop(0, kv_heads // 2, prepare, 0)
+    if half > 1:
+        pass_on(0)
+    lax.fori_loop(kv_heads // 2, kv_heads, prepare, 0)
 
     def unit(key_tile, value_tile, g, a, masked):
         queries, grads = qs[g, a], gs[g, a]
         scores = dot_rows(key_tile, queries)
-        weights = jnp.exp2(scores * (scaling * LOG2E) - lse_ref[g, a])
+        weights = jnp.exp2(scores * (scaling * LOG2E) - lse[g, a])
         if masked:
             key_row = lax.broadcasted_iota(jnp.int32, (rows, wide), 0)
             query_row = lax.broadcasted_iota(jnp.int32, (rows, wide), 1) % rows
@@ -174,43 +189,29 @@
 
         lax.fori_loop(0, kv_heads, head, 0)
 
-    def receive(distance):
-        gather_copy(RIGHT, KEYS, distance, False).wait_recv()
-        gather_copy(LEFT, VALUES, distance, False).wait_recv()
-        gather_copy(RIGHT, VALUES, distance, False).wait_recv()
-        gather_copy(LEFT, KEYS, distance, False).wait_recv()
+    def send_sum(what, step, block, first):
+        if not first:
+            slot = n - 1 - step if what == KEYS else 1 + step
+            sum_copy(what, step - 1, block).wait_recv()
+            part[what, slot, block] += landed[what, step - 1, block]
+        sum_copy(what, step, block).start()
 
     def send_sums(step, first):
         for block in range(2):
             for what in (KEYS, VALUES):
-                if not first:
-                    slot = n - 1 - step if what == KEYS else 1 + step
-                    sum_copy(what, step - 1, block).wait_recv()
-                    part[what, slot, block] += landed[what, step - 1, block]
-                sum_copy(what, step, block).start()
+                send_sum(what, step, block, first)
 
     def near(step, first):
-        receive(step + 1)
-
-        gather_copy(RIGHT, KEYS, step + 2, False).start()
-        gather_copy(LEFT, VALUES, step + 2, False).start()
-
-        @pl.when(step + 2 < half)
-        def _():
-            gather_copy(RIGHT, VALUES, step + 2, False).start()
-            gather_copy(LEFT, KEYS, step + 2, False).start()
-
-        def side(which, _):
-            shard(jnp.where(which == 0, n - 1 - step, 1 + step))
-            return 0
-
-        lax.fori_loop(0, 2, side, 0)
-        send_sums(step, first)
+        for what in (KEYS, VALUES):
+            shard(n - 1 - step if what == KEYS else 1 + step)
+            for block in range(2):
+                send_sum(what, step, block, first)
 
     if half > 1:
         near(0, True)
 
         def middle(step, _):
+            pass_on(step)
             near(step, False)
             return 0
 
@@ -223,6 +224,9 @@
 
     own_shard()
     for a in range(2):
+        if half + a < n - 1:
+            send_sums(half + a, False)
+
         def write(g, _):
             turned = jnp.transpose(dqt[g, a]) * scaling
             for j in range(group):
@@ -236,7 +240,7 @@
         send_sums(step, False)
         return 0
 
-    lax.fori_loop(half, n - 1, far, 0)
+    lax.fori_loop(half + 2, n - 1, far, 0)
     for block in range(2):
         for what in (KEYS, VALUES):
             sum_copy(what, n - 2, block).wait_recv()
@@ -272,8 +276,9 @@
     kv_heads = keys.shape[3] // HEAD_SIZE
     group = queries.shape[3] // keys.shape[3]
     wide = group * rows
-    lse = logsumexp[0].reshape(2, rows, kv_heads, group).transpose(2, 0, 3, 1)
-    lse = (lse * LOG2E).reshape(kv_heads, 2, 1, wide)
+    lse = logsumexp.transpose(0, 1, 3, 2)
+    shard_bytes = 2 * 2 * rows * keys.shape[3]
+    limit = (20 << 20) + n * shard_bytes * 10
     vmem = pl.BlockSpec(memory_space=pltpu.VMEM)
     pair = (2, rows, keys.shape[3])
     return pl.pallas_call(
@@ -289,6 +294,7 @@
             pltpu.VMEM((kv_heads, 2, wide, HEAD_SIZE), jnp.bfloat16),
             pltpu.VMEM((kv_heads, 2, wide, HEAD_SIZE), jnp.bfloat16),
             pltpu.VMEM((kv_heads, 2, 1, wide), jnp.float32),
+            pltpu.VMEM((kv_heads, 2, 1, wide), jnp.float32),
             pltpu.VMEM((kv_heads, 2, HEAD_SIZE, wide), jnp.float32),
             pltpu.VMEM((n, 2) + pair, jnp.bfloat16),
             pltpu.VMEM((2, n) + pair, jnp.float32),
@@ -299,7 +305,7 @@
             pltpu.SemaphoreType.DMA((2, n - 1, 2)),
         ],
         compiler_params=pltpu.CompilerParams(
-            collective_id=0, has_side_effects=True, vmem_limit_bytes=64_000_000
+            collective_id=0, has_side_effects=True, vmem_limit_bytes=limit
         ),
     )(queries, keys, values, output, gradient, lse)
 

time: 81.3 us -> 81.6 us (level)
  local copies, waits for them, and re-layouts: 5.27 us -> 8.96 us
  Pallas kernels: 74.4 us -> 71.6 us
    unnamed x7 -> x15, local copies, waits for them, and re-layouts: 4.58 us -> 8.96 us
    pallas_call x1, Pallas kernels: 74.4 us -> 71.6 us  [body(): pl.pallas_call(functools.partial(kernel, n), out_shape=(jax.ShapeDtypeStr...]
where the time goes in v2:
time: 81.6 us; the launch traced here: 81.2 us
  Pallas kernels  71.6 us (88%)
  local copies, waits for them, and re-layouts  8.96 us (11%)
    pallas_call x1, Pallas kernels, body(): pl.pallas_call(functools.partial(kernel, n), out_shape=(jax.ShapeDtypeStr...  71.6 us
    unnamed x15, local copies, waits for them, and re-layouts  8.96 us

profile of v2, /device:TPU:0, one launch (start us, length us, event | category | flops | bytes accessed | tf_op | source)
XLA Modules:
  0.0 81.2 jit_solution(9085408942442659280)
XLA Ops:
  0.6 0.0 copy-start
  0.6 1.2 %copy-done = bf16[1,2,64,4096]{3,2,1,0:T(8,128)(2,1)S(1)} copy-done((bf16[1,2,64,4096]{3,2,1,0:T(8,128)(2,1)S(1)}, bf16[1,2,64,4096]{3,2,1,0:T(8,128)(2,1)}, u32[]{:S(2)}) %copy-start) | copy-done | bytes 1048600
  1.9 0.0 copy-start.1
  1.9 1.2 %copy-done.1 = bf16[1,2,64,4096]{3,2,1,0:T(8,128)(2,1)S(1)} copy-done((bf16[1,2,64,4096]{3,2,1,0:T(8,128)(2,1)S(1)}, bf16[1,2,64,4096]{3,2,1,0:T(8,128)(2,1)}, u32[]{:S(2)}) %copy-start.1) | copy-done | bytes 1048600
  3.1 0.0 copy-start.2
  3.1 1.2 %copy-done.2 = bf16[1,2,64,4096]{3,2,1,0:T(8,128)(2,1)S(1)} copy-done((bf16[1,2,64,4096]{3,2,1,0:T(8,128)(2,1)S(1)}, bf16[1,2,64,4096]{3,2,1,0:T(8,128)(2,1)}, u32[]{:S(2)}) %copy-start.2) | copy-done | bytes 1048600
  4.3 0.0 copy-start.3
  4.3 0.9 %copy-done.3 = bf16[1,2,64,512]{3,2,1,0:T(8,128)(2,1)S(1)} copy-done((bf16[1,2,64,512]{3,2,1,0:T(8,128)(2,1)S(1)}, bf16[1,2,64,512]{3,2,1,0:T(8,128)(2,1)}, u32[]{:S(2)}) %copy-start.3) | copy-done | bytes 131096
  5.2 0.0 copy-start.4
  5.2 0.9 %copy-done.4 = bf16[1,2,64,512]{3,2,1,0:T(8,128)(2,1)S(1)} copy-done((bf16[1,2,64,512]{3,2,1,0:T(8,128)(2,1)S(1)}, bf16[1,2,64,512]{3,2,1,0:T(8,128)(2,1)}, u32[]{:S(2)}) %copy-start.4) | copy-done | bytes 131096
  6.1 0.0 copy-start.5
  6.1 0.8 copy-done.5
  6.9 71.6 %shard_map.85 = (f32[1,2,64,4096]{3,2,1,0:T(8,128)S(1)}, f32[1,2,64,512]{3,2,1,0:T(8,128)S(1)}, f32[1,2,64,512]{3,2,1,0:T(8,128)S(1)}) custom-call(bf16[1,2,64,4096]{3,2,1,0:T(8,128)(2,1)S(1)} %copy-done, bf16[1,2,64,512]{3,2,1,0:T(8,128)(2,1)S(1)} %copy-done.3, bf16[1,2,64,512]{3,2,1,0:T(8,128)(2,1)S(1)} %copy-done.4, ...), custom_call_target="tpu_custom_call" | custom-call | tf_op jit(solution)/shard_map/pallas_call | solution.py:284
  78.5 1.3 %copy.12 = f32[1,2,64,4096]{3,2,1,0:T(8,128)} copy(f32[1,2,64,4096]{3,2,1,0:T(8,128)S(1)} %get-tuple-element.6) | data formatting | bytes 4194304
  79.8 0.7 copy.13
  80.5 0.7 copy.14
Async XLA Ops:
  0.6 1.2 %copy-start = (bf16[1,2,64,4096]{3,2,1,0:T(8,128)(2,1)S(1)}, bf16[1,2,64,4096]{3,2,1,0:T(8,128)(2,1)}, u32[]{:S(2)}) copy-start(bf16[1,2,64,4096]{3,2,1,0:T(8,128)(2,1)} %q_ref.1) | copy-start | bytes 3145732
  1.9 1.2 %copy-start.1 = (bf16[1,2,64,4096]{3,2,1,0:T(8,128)(2,1)S(1)}, bf16[1,2,64,4096]{3,2,1,0:T(8,128)(2,1)}, u32[]{:S(2)}) copy-start(bf16[1,2,64,4096]{3,2,1,0:T(8,128)(2,1)} %o_ref.1) | copy-start | bytes 3145732
  3.1 1.2 %copy-start.2 = (bf16[1,2,64,4096]{3,2,1,0:T(8,128)(2,1)S(1)}, bf16[1,2,64,4096]{3,2,1,0:T(8,128)(2,1)}, u32[]{:S(2)}) copy-start(bf16[1,2,64,4096]{3,2,1,0:T(8,128)(2,1)} %g_ref.1) | copy-start | bytes 3145732
  4.3 0.9 %copy-start.3 = (bf16[1,2,64,512]{3,2,1,0:T(8,128)(2,1)S(1)}, bf16[1,2,64,512]{3,2,1,0:T(8,128)(2,1)}, u32[]{:S(2)}) copy-start(bf16[1,2,64,512]{3,2,1,0:T(8,128)(2,1)} %k_ref.1) | copy-start | bytes 393220
  5.2 0.9 %copy-start.4 = (bf16[1,2,64,512]{3,2,1,0:T(8,128)(2,1)S(1)}, bf16[1,2,64,512]{3,2,1,0:T(8,128)(2,1)}, u32[]{:S(2)}) copy-start(bf16[1,2,64,512]{3,2,1,0:T(8,128)(2,1)} %v_ref.1) | copy-start | bytes 393220
  6.1 0.8 copy-start.5
